TPU v7x, 32 devices: a whole 2x2x4 slice. The times are simulated.
32 devices in a mesh: seq: 8 (over z, core), fsdp: 4 (over y, x).
Axes of the slice: x: 2, y: 2, z: 4, core: 2. Of those that a mesh axis runs over, the one named last changes fastest.
Arguments:
- tokens: bfloat16 [4, 1024, 2048], P('fsdp', 'seq'), may hold values from -6 to 6
- ln_gain: bfloat16 [2048], P('fsdp'), may hold values from 0.5 to 1.5
- ln_bias: bfloat16 [2048], P('fsdp'), may hold values from -3 to 3
- qkv_weight: bfloat16 [2048, 6144], P('fsdp')
- qkv_bias: bfloat16 [6144], P('fsdp'), may hold values from -3 to 3
- dense_weight: bfloat16 [2048, 2048], P('fsdp'), may hold values from -0.5 to 0.5
- dense_bias: bfloat16 [2048], P('fsdp'), may hold values from -3 to 3
- fc1_weight: bfloat16 [2048, 8192], P('fsdp'), may hold values from -0.125 to 0.125
- fc1_bias: bfloat16 [8192], P('fsdp'), may hold values from -3 to 3
- fc2_weight: bfloat16 [8192, 2048], P('fsdp'), may hold values from -0.0625 to 0.0625
- fc2_bias: bfloat16 [2048], P('fsdp'), may hold values from -3 to 3
- segments: int32 [4, 1024], P('fsdp'), may hold values from 0 to 1, as said below
- positions: int32 [4, 1024], P('fsdp', 'seq'), may hold values from 0 to 2046, as said below
- cotangent: bfloat16 [4, 1024, 2048], P('fsdp', 'seq'), may hold values from -6 to 6
Outputs:
- out: bfloat16 [4, 1024, 2048], P('fsdp', 'seq')
- grad_tokens: float32 [4, 1024, 2048], P('fsdp', 'seq')
- grad_ln_gain: float32 [2048], P('fsdp')
- grad_ln_bias: float32 [2048], P('fsdp')
- grad_qkv_weight: float32 [2048, 6144], P('fsdp')
- grad_qkv_bias: float32 [6144], P('fsdp')
- grad_dense_weight: float32 [2048, 2048], P('fsdp')
- grad_dense_bias: float32 [2048], P('fsdp')
- grad_fc1_weight: float32 [2048, 8192], P('fsdp')
- grad_fc1_bias: float32 [8192], P('fsdp')
- grad_fc2_weight: float32 [8192, 2048], P('fsdp')
- grad_fc2_bias: float32 [2048], P('fsdp')
Inputs may be any that keep to these rules, and one draw needn't show every extreme that they name: `segments`: document numbers never fall along a sequence and each of 0 to 1 occurs in every sequence. The first document of each sequence starts at position 0; positions rise by one from token to token within a document; in every sequence the last token of the last document has position 2046.
All inputs are finite; a program needn't handle non-finite values.
Results may differ from a plain program's by a relative error of at most 0.0095.
Values may be sent and summed in bfloat16 or wider, within the bound.
A program may use at most 448 MiB of HBM per device.

v0:
```python
import jax
import jax.numpy as jnp
from jax import lax
from jax.sharding import PartitionSpec as P

HEADS = 32
HEAD = 64
ROT = 32
norm_epsilon = 1e-05


def rotary_angles(pos_row, rot_width):
    inverse = 1.0 / 10000.0 ** (jnp.arange(0, rot_width, 2, dtype=jnp.float32) / rot_width)
    return pos_row.astype(jnp.float32)[:, None] * inverse[None, :]


def rotate_pair(values_in, angles):
    half_width = angles.shape[-1]
    cosine = jnp.cos(angles)[:, None, None, :]
    sine_part = jnp.sin(angles)[:, None, None, :]
    low_half = values_in[..., :half_width]
    high_half = values_in[..., half_width : 2 * half_width]
    rest_part = values_in[..., 2 * half_width :]
    return jnp.concatenate(
        [
            low_half * cosine - high_half * sine_part,
            high_half * cosine + low_half * sine_part,
            rest_part,
        ],
        axis=-1,
    )


def gelu_tanh(values_in):
    return jax.nn.gelu(values_in, approximate=True)


def contract_rows(left_side, right_side):
    return lax.dot_general(
        left_side, right_side, (((0,), (0,)), ((), ())), preferred_element_type=jnp.float32
    )


def contract_cols(left_side, right_side):
    return lax.dot_general(
        left_side, right_side, (((1,), (1,)), ((), ())), preferred_element_type=jnp.float32
    )


def block_scores(query_block, keys_all, first_row, seg_row):
    block_len = query_block.shape[0]
    seq_len = keys_all.shape[0]
    score_scale = query_block.shape[2] ** (-0.5)
    scores = (
        jnp.einsum("qhd,khd->hqk", query_block, keys_all, preferred_element_type=jnp.float32)
        * score_scale
    )
    query_place = first_row + jnp.arange(block_len)
    key_place = jnp.arange(seq_len)
    query_seg = lax.dynamic_slice_in_dim(seg_row, first_row, block_len, 0)
    allowed = (key_place[None, :] <= query_place[:, None]) & (
        query_seg[:, None] == seg_row[None, :]
    )
    return (jnp.where(allowed[None], scores, -1e30), allowed)


def attend_forward(queries, keys_all, values, seg_row):
    seq_len = queries.shape[0]
    block_len = min(512, seq_len)
    count_blocks = seq_len // block_len

    def one_block(block_index):
        first_row = block_index * block_len
        query_block = lax.dynamic_slice_in_dim(queries, first_row, block_len, 0)
        scores, allowed = block_scores(query_block, keys_all, first_row, seg_row)
        row_top = jnp.max(scores, axis=-1, keepdims=True)
        raised = jnp.exp(scores - row_top)
        row_total = jnp.sum(raised, axis=-1, keepdims=True)
        probabilities = raised / row_total
        result = jnp.einsum(
            "hqk,khd->qhd",
            probabilities.astype(jnp.bfloat16),
            values,
            preferred_element_type=jnp.float32,
        )
        return (result, row_top[..., 0] + jnp.log(row_total[..., 0]))

    outputs, log_norm = lax.map(one_block, jnp.arange(count_blocks))
    return (outputs.reshape(seq_len, queries.shape[1], queries.shape[2]), log_norm)


def attend_backward(queries, keys_all, values, seg_row, log_norm, grad_out):
    seq_len = queries.shape[0]
    block_len = min(512, seq_len)
    count_blocks = seq_len // block_len
    score_scale = queries.shape[2] ** (-0.5)

    def one_block(running, block_index):
        grad_keys, grad_values = running
        first_row = block_index * block_len
        query_block = lax.dynamic_slice_in_dim(queries, first_row, block_len, 0)
        grad_block = lax.dynamic_slice_in_dim(grad_out, first_row, block_len, 0)
        scores, allowed = block_scores(query_block, keys_all, first_row, seg_row)
        probabilities = jnp.where(
            allowed[None], jnp.exp(scores - log_norm[block_index][..., None]), 0.0
        )
        grad_probs = jnp.einsum(
            "qhd,khd->hqk", grad_block, values, preferred_element_type=jnp.float32
        )
        row_inner = jnp.sum(probabilities * grad_probs, axis=-1, keepdims=True)
        grad_scores = (probabilities * (grad_probs - row_inner)).astype(jnp.bfloat16)
        grad_query = (
            jnp.einsum("hqk,khd->qhd", grad_scores, keys_all, preferred_element_type=jnp.float32)
            * score_scale
        )
        grad_keys = (
            grad_keys
            + jnp.einsum(
                "hqk,qhd->khd", grad_scores, query_block, preferred_element_type=jnp.float32
            )
            * score_scale
        )
        grad_values = grad_values + jnp.einsum(
            "hqk,qhd->khd",
            probabilities.astype(jnp.bfloat16),
            grad_block,
            preferred_element_type=jnp.float32,
        )
        return ((grad_keys, grad_values), grad_query)

    zeros_start = jnp.zeros(keys_all.shape, jnp.float32)
    (grad_keys, grad_values), grad_queries = lax.scan(
        one_block, (zeros_start, zeros_start), jnp.arange(count_blocks)
    )
    return (grad_queries.reshape(queries.shape), grad_keys, grad_values)


def body(
    tokens,
    ln_gain,
    ln_bias,
    qkv_weight,
    qkv_bias,
    dense_weight,
    dense_bias,
    fc1_weight,
    fc1_bias,
    fc2_weight,
    fc2_bias,
    segments,
    positions,
    cotangent,
):
    seq_count = lax.axis_size("seq")
    shard_count = lax.axis_size("fsdp")
    gathered = (
        lax.all_gather(qkv_weight, "fsdp", axis=0, tiled=True),
        lax.all_gather(dense_weight, "fsdp", axis=0, tiled=True),
        lax.all_gather(fc1_weight, "fsdp", axis=0, tiled=True),
        lax.all_gather(fc2_weight, "fsdp", axis=0, tiled=True),
        lax.all_gather(ln_gain, "fsdp", axis=0, tiled=True),
        lax.all_gather(ln_bias, "fsdp", axis=0, tiled=True),
        lax.all_gather(qkv_bias, "fsdp", axis=0, tiled=True),
        lax.all_gather(dense_bias, "fsdp", axis=0, tiled=True),
        lax.all_gather(fc1_bias, "fsdp", axis=0, tiled=True),
        lax.all_gather(fc2_bias, "fsdp", axis=0, tiled=True),
    )
    w_qkv, w_dense, w_up, w_down = (gathered[0], gathered[1], gathered[2], gathered[3])
    gain_full, shift_full, b_qkv, b_dense, b_up, b_down = (
        gathered[4],
        gathered[5],
        gathered[6],
        gathered[7],
        gathered[8],
        gathered[9],
    )
    tok_len = tokens.shape[1]
    model_width = tokens.shape[2]
    heads_here = HEADS // seq_count
    head_slab = heads_here * HEAD
    inputs = tokens[0].astype(jnp.float32)
    centre = jnp.mean(inputs, axis=-1, keepdims=True)
    variance = jnp.mean((inputs - centre) ** 2, axis=-1, keepdims=True)
    inv_std = lax.rsqrt(variance + norm_epsilon)
    standard = (inputs - centre) * inv_std
    normed = (standard * gain_full.astype(jnp.float32) + shift_full.astype(jnp.float32)).astype(
        jnp.bfloat16
    )
    projected = jnp.dot(normed, w_qkv, preferred_element_type=jnp.float32) + b_qkv.astype(
        jnp.float32
    )
    projected = projected.reshape(tok_len, 3, HEADS, HEAD)
    angles = rotary_angles(positions[0], ROT)
    turned = jnp.concatenate(
        [rotate_pair(projected[:, :2], angles), projected[:, 2:]], axis=1
    ).astype(jnp.bfloat16)
    outgoing = turned.reshape(tok_len, 3, seq_count, head_slab)
    by_heads = lax.all_to_all(outgoing, "seq", split_axis=2, concat_axis=0, tiled=True)
    seq_len = by_heads.shape[0]
    by_heads = by_heads.reshape(seq_len, 3, heads_here, HEAD)
    queries, keys_all, values = (by_heads[:, 0], by_heads[:, 1], by_heads[:, 2])
    seg_row = segments[0]
    attended, log_norm = attend_forward(queries, keys_all, values, seg_row)
    returned_heads = lax.all_to_all(
        attended.astype(jnp.bfloat16).reshape(seq_len, 1, head_slab),
        "seq",
        split_axis=0,
        concat_axis=1,
        tiled=True,
    )
    att_tokens = returned_heads.reshape(tok_len, model_width)
    branch_att = jnp.dot(att_tokens, w_dense, preferred_element_type=jnp.float32) + b_dense.astype(
        jnp.float32
    )
    pre_act = jnp.dot(normed, w_up, preferred_element_type=jnp.float32) + b_up.astype(jnp.float32)
    activated = gelu_tanh(pre_act).astype(jnp.bfloat16)
    branch_mlp = jnp.dot(activated, w_down, preferred_element_type=jnp.float32) + b_down.astype(
        jnp.float32
    )
    result = (inputs + branch_att + branch_mlp).astype(jnp.bfloat16)
    regathered = (
        lax.all_gather(qkv_weight, "fsdp", axis=0, tiled=True),
        lax.all_gather(dense_weight, "fsdp", axis=0, tiled=True),
        lax.all_gather(fc1_weight, "fsdp", axis=0, tiled=True),
        lax.all_gather(fc2_weight, "fsdp", axis=0, tiled=True),
        lax.all_gather(ln_gain, "fsdp", axis=0, tiled=True),
        lax.all_gather(ln_bias, "fsdp", axis=0, tiled=True),
        lax.all_gather(qkv_bias, "fsdp", axis=0, tiled=True),
        lax.all_gather(dense_bias, "fsdp", axis=0, tiled=True),
        lax.all_gather(fc1_bias, "fsdp", axis=0, tiled=True),
        lax.all_gather(fc2_bias, "fsdp", axis=0, tiled=True),
    )
    w_qkv, w_dense, w_up, w_down = (regathered[0], regathered[1], regathered[2], regathered[3])
    gain_full = regathered[4]
    upstream = cotangent[0]
    grad_act = contract_cols(upstream, w_down)
    grad_slope = jax.vjp(gelu_tanh, pre_act)[1](grad_act)[0]
    grad_pre = grad_slope.astype(jnp.bfloat16)
    grad_att = contract_cols(upstream, w_dense).astype(jnp.bfloat16)
    heads_grad = lax.all_to_all(
        grad_att.reshape(tok_len, seq_count, head_slab),
        "seq",
        split_axis=1,
        concat_axis=0,
        tiled=True,
    )
    heads_grad = heads_grad.reshape(seq_len, heads_here, HEAD)
    grad_q, grad_k, grad_v = attend_backward(
        queries, keys_all, values, seg_row, log_norm, heads_grad
    )
    stacked = (
        jnp.stack([grad_q, grad_k, grad_v], axis=1)
        .astype(jnp.bfloat16)
        .reshape(seq_len, 3, 1, head_slab)
    )
    returned = lax.all_to_all(stacked, "seq", split_axis=0, concat_axis=2, tiled=True)
    returned = returned.reshape(tok_len, 3, HEADS, HEAD).astype(jnp.float32)
    unturned = jnp.concatenate([rotate_pair(returned[:, :2], -angles), returned[:, 2:]], axis=1)
    grad_mixed = unturned.reshape(tok_len, 3 * model_width).astype(jnp.bfloat16)
    grad_normed = contract_cols(grad_mixed, w_qkv) + contract_cols(grad_pre, w_up)
    scaled = grad_normed * gain_full.astype(jnp.float32)
    grad_inputs = upstream.astype(jnp.float32) + inv_std * (
        scaled
        - jnp.mean(scaled, axis=-1, keepdims=True)
        - standard * jnp.mean(scaled * standard, axis=-1, keepdims=True)
    )
    gain_term = jnp.sum(grad_normed * standard, axis=0)
    shift_term = jnp.sum(grad_normed, axis=0)
    qkv_term = jnp.sum(grad_mixed.astype(jnp.float32), axis=0)
    out_term = jnp.sum(upstream.astype(jnp.float32), axis=0)
    up_term = jnp.sum(grad_pre.astype(jnp.float32), axis=0)

    def spread_vec(vector):
        return vector.reshape(shard_count, seq_count, -1).transpose(1, 0, 2).reshape(-1)

    vector_parts = (
        lax.psum_scatter(spread_vec(gain_term), ("seq", "fsdp"), scatter_dimension=0, tiled=True),
        lax.psum_scatter(spread_vec(shift_term), ("seq", "fsdp"), scatter_dimension=0, tiled=True),
        lax.psum_scatter(spread_vec(qkv_term), ("seq", "fsdp"), scatter_dimension=0, tiled=True),
        lax.psum_scatter(spread_vec(out_term), ("seq", "fsdp"), scatter_dimension=0, tiled=True),
        lax.psum_scatter(spread_vec(up_term), ("seq", "fsdp"), scatter_dimension=0, tiled=True),
    )
    ff_width = w_up.shape[1]
    col_qkv = 3 * model_width // seq_count
    col_up = ff_width // seq_count
    row_dense = model_width // (shard_count * seq_count)
    row_down = ff_width // (shard_count * seq_count)
    normed_full, upstream_full = (
        lax.all_gather(normed, "seq", axis=0, tiled=True),
        lax.all_gather(upstream, "seq", axis=0, tiled=True),
    )
    grads_cols = (
        lax.all_to_all(
            grad_mixed.reshape(tok_len, seq_count, col_qkv),
            "seq",
            split_axis=1,
            concat_axis=0,
            tiled=True,
        ),
        lax.all_to_all(
            grad_pre.reshape(tok_len, seq_count, col_up),
            "seq",
            split_axis=1,
            concat_axis=0,
            tiled=True,
        ),
    )
    mixed_cols = grads_cols[0].reshape(seq_len, col_qkv)
    pre_cols = grads_cols[1].reshape(seq_len, col_up)
    rows_sel = (
        lax.all_to_all(
            att_tokens.reshape(tok_len, shard_count, seq_count, row_dense),
            "seq",
            split_axis=2,
            concat_axis=0,
            tiled=True,
        ),
        lax.all_to_all(
            activated.reshape(tok_len, shard_count, seq_count, row_down),
            "seq",
            split_axis=2,
            concat_axis=0,
            tiled=True,
        ),
    )
    att_sel = rows_sel[0].reshape(seq_len, shard_count * row_dense)
    down_sel = rows_sel[1].reshape(seq_len, shard_count * row_down)

    def moved_sum(left_full, right_side):
        return lax.psum_scatter(
            contract_rows(left_full, right_side).astype(jnp.bfloat16),
            "fsdp",
            scatter_dimension=0,
            tiled=True,
        ).astype(jnp.float32)

    piece_qkv = moved_sum(normed_full, mixed_cols)
    piece_dense = moved_sum(att_sel, upstream_full)
    piece_up = moved_sum(normed_full, pre_cols)
    piece_down = moved_sum(down_sel, upstream_full)
    reduced = (
        lax.all_gather(piece_qkv.astype(jnp.bfloat16), "seq", axis=1, tiled=True).astype(
            piece_qkv.dtype
        ),
        lax.all_gather(piece_dense.astype(jnp.bfloat16), "seq", axis=0, tiled=True).astype(
            piece_dense.dtype
        ),
        lax.all_gather(piece_up.astype(jnp.bfloat16), "seq", axis=1, tiled=True).astype(
            piece_up.dtype
        ),
        lax.all_gather(piece_down.astype(jnp.bfloat16), "seq", axis=0, tiled=True).astype(
            piece_down.dtype
        ),
        lax.all_gather(vector_parts[0].astype(jnp.bfloat16), "seq", axis=0, tiled=True).astype(
            jnp.float32
        ),
        lax.all_gather(vector_parts[1].astype(jnp.bfloat16), "seq", axis=0, tiled=True).astype(
            jnp.float32
        ),
        lax.all_gather(vector_parts[2].astype(jnp.bfloat16), "seq", axis=0, tiled=True).astype(
            jnp.float32
        ),
        lax.all_gather(vector_parts[3].astype(jnp.bfloat16), "seq", axis=0, tiled=True).astype(
            jnp.float32
        ),
        lax.all_gather(vector_parts[4].astype(jnp.bfloat16), "seq", axis=0, tiled=True).astype(
            jnp.float32
        ),
    )
    return (
        result[None],
        grad_inputs[None],
        reduced[4],
        reduced[5],
        reduced[0],
        reduced[6],
        reduced[1],
        reduced[7],
        reduced[2],
        reduced[8],
        reduced[3],
        reduced[7],
    )


def solution(mesh):
    return jax.shard_map(
        body,
        mesh=mesh,
        in_specs=(
            P("fsdp", "seq", None),
            P("fsdp"),
            P("fsdp"),
            P("fsdp", None),
            P("fsdp"),
            P("fsdp", None),
            P("fsdp"),
            P("fsdp", None),
            P("fsdp"),
            P("fsdp", None),
            P("fsdp"),
            P("fsdp", None),
            P("fsdp", "seq"),
            P("fsdp", "seq", None),
        ),
        out_specs=(
            P("fsdp", "seq", None),
            P("fsdp", "seq", None),
            P("fsdp"),
            P("fsdp"),
            P("fsdp", None),
            P("fsdp"),
            P("fsdp", None),
            P("fsdp"),
            P("fsdp", None),
            P("fsdp"),
            P("fsdp", None),
            P("fsdp"),
        ),
        check_vma=False,
    )
```

profile of v0, /device:TPU:0, one launch (start us, length us, event | category | flops | bytes accessed | tf_op | source)
XLA Modules:
  0.0 1528.9 jit_solution(6657508894019280868)
XLA Ops:
  39.4 60.9 %all-gather.20.cloned.1.call-done = bf16[2048,2048]{1,0:T(8,128)(2,1)} async-done(((bf16[512,2048]{1,0:T(8,128)(2,1)}), bf16[2048,2048]{1,0:T(8,128)(2,1)}) %all-gather.20.cloned.1.call-update) | async-done | bytes 8388624 | tf_op jit(solution)/shard_map/all_gather | solution.py:158
  112.0 217.8 %all-gather.18.cloned.1.call-done = bf16[2048,6144]{1,0:T(8,128)(2,1)} async-done(((bf16[512,6144]{1,0:T(8,128)(2,1)}), bf16[2048,6144]{1,0:T(8,128)(2,1)}) %all-gather.18.cloned.1.call-update) | async-done | bytes 25165840 | tf_op jit(solution)/shard_map/all_gather | solution.py:157
  329.8 13.3 convolution_add_fusion.1
  354.1 56.5 %all-to-all-done = bf16[128,3,8,256]{0,3,1,2:T(8,128)(2,1)} async-done(((bf16[128,3,8,256]{0,3,1,2:T(8,128)(2,1)}), bf16[128,3,8,256]{0,3,1,2:T(8,128)(2,1)}, u32[]{:S(2)}, u32[]{:S(2)}) %all-to-all-start) | async-done | bytes 1572896 | tf_op jit(solution)/shard_map/all_to_all | solution.py:198
  421.2 20.8 %while.27 = (s32[]{:T(128)}, bf16[2,512,4,64]{1,3,2,0:T(8,128)(2,1)}, f32[2,4,512]{2,1,0:T(4,128)S(1)}, s32[2]{0:T(128)S(1)}, s32[1024]{0:T(1024)S(1)}, /*index=...) while((s32[]{:T(128)}, ...), condition=%wide.region_5.6_spmd, body=%wide.region_2.5_spmd.sunk | while | flops 563608064 | bytes 31275748 | solution.py:88
  462.7 61.2 %while.28 = (s32[]{:T(128)}, f32[1024,4,64]{0,2,1:T(8,128)S(1)}, f32[1024,4,64]{0,2,1:T(8,128)S(1)}, bf16[2,512,4,64]{1,3,2,0:T(8,128)(2,1)}, s32[2]{0:T(128)S(1...) while((s32[]{:T(128)}, f32[1024,4,64]{0,2,1:T(8,128)S(1)}, ...), condition=%wide.region_8.9_spmd.clone, body=%wide.region_6.8_spmd.clone.sunk | while | flops 1366161920 | bytes 180411312 | solution.py:132
  539.1 43.7 %all-to-all-done.3 = bf16[1024,3,1,256]{3,1,2,0:T(4,128)(2,1)S(1)} async-done(((bf16[1024,3,1,256]{3,1,2,0:T(4,128)(2,1)}), bf16[1024,3,1,256]{3,1,2,0:T(4,128)(2,1)S(1)}, u32[]{:S(2)}, u32[]{:S(2)}) %all-to-all-start.3) | async-done | bytes 1572896 | tf_op jit(solution)/shard_map/all_to_all | solution.py:256
  620.7 22.9 %all-to-all-done.4 = bf16[128,8,768]{0,2,1:T(8,128)(2,1)S(1)} async-done(((bf16[128,8,768]{0,2,1:T(8,128)(2,1)}), bf16[128,8,768]{0,2,1:T(8,128)(2,1)S(1)}, u32[]{:S(2)}, u32[]{:S(2)}) %all-to-all-start.4) | async-done | bytes 1572896 | tf_op jit(solution)/shard_map/all_to_all | solution.py:293
  651.9 99.4 %all-gather.22.cloned.1.call-done = bf16[2048,8192]{1,0:T(8,128)(2,1)} async-done(((bf16[512,8192]{1,0:T(8,128)(2,1)}), bf16[2048,8192]{1,0:T(8,128)(2,1)}) %all-gather.22.cloned.1.call-update) | async-done | bytes 33554448 | tf_op jit(solution)/shard_map/all_gather | solution.py:159
  751.3 19.0 %multiply_convert_fusion.1 = (bf16[128,8192]{1,0:T(8,128)(2,1)}, f32[128,8192]{1,0:T(8,128)}) fusion(f32[8192]{0:T(1024)S(1)} %convert_element_type.189, bf16[128,2048]{1,0:T(8,128)(2,1)S(1)} %copy-done.10, bf16[2048,8192]{1,0:T(8,128)(2,1)} %all-gather.22.cloned.1.call-done), kind=kOutput, calls=%fused_computation.59 | convolution fusion | flops 4305453056 | bytes 40402944 | tf_op jit(solution)/shard_map/dot_general | solution.py:215
  770.3 279.8 %all-gather.24.cloned.1.call-done = bf16[8192,2048]{1,0:T(8,128)(2,1)} async-done(((bf16[2048,2048]{1,0:T(8,128)(2,1)}), bf16[8192,2048]{1,0:T(8,128)(2,1)}) %all-gather.24.cloned.1.call-update) | async-done | bytes 33554448 | tf_op jit(solution)/shard_map/all_gather | solution.py:160
  1050.1 18.0 %convert_reduce_fusion = (f32[8192]{0:T(1024)S(1)}, bf16[128,8192]{1,0:T(8,128)(2,1)S(1)}) fusion(f32[128,8192]{1,0:T(8,128)} %get-tuple-element.255, bf16[8192,2048]{1,0:T(8,128)(2,1)} %all-gather.24.cloned.1.call-done, bf16[1,128,2048]{2,1,0:T(8,128)(2,1)S(1)} %copy-done.12), kind=kOutput, calls=%fused_computation.58 | convolution fusion | flops 4318027776 | bytes 40402944 | tf_op jit(solution)/shard_map/dot_general | solution.py:45
  1068.3 53.7 %all_to_all.114 = bf16[128,8,1024]{2,0,1:T(8,128)(2,1)S(1)} all-to-all(bf16[128,8,1024]{2,0,1:T(8,128)(2,1)S(1)} %bitcast.256), channel_id=1, replica_groups=mesh['seq'=8,'fsdp'=4] {'seq'}, dimensions={1} | all-to-all | bytes 4194304 | tf_op jit(solution)/shard_map/all_to_all | solution.py:300
  1136.4 53.1 %all_to_all.115 = bf16[128,4,8,256]{0,3,1,2:T(8,128)(2,1)S(1)} all-to-all(bf16[128,4,8,256]{0,3,1,2:T(8,128)(2,1)} %copy.127), channel_id=1, replica_groups=mesh['seq'=8,'fsdp'=4] {'seq'}, dimensions={2} | all-to-all | bytes 4194304 | tf_op jit(solution)/shard_map/all_to_all | solution.py:318
  1199.1 48.6 %reduce-scatter.11.cloned.1.call-done = bf16[256,2048]{1,0:T(8,128)(2,1)} async-done(((bf16[1024,2048]{1,0:T(8,128)(2,1)}), bf16[256,2048]{1,0:T(8,128)(2,1)}) %reduce-scatter.11.cloned.1.call-update) | async-done | bytes 1048592 | tf_op jit(solution)/shard_map/reduce_scatter | solution.py:330
  1270.8 14.3 fusion.80
  1289.5 17.7 %fusion.68 = (f32[2048]{0:T(1024)S(1)}, f32[128]{0:T(128)S(1)}, f32[128]{0:T(128)S(1)}, f32[2048]{0:T(1024)S(1)}, f32[128,2048]{1,0:T(8,128)}) fusion(bf16[1,128,2048]{2,1,0:T(8,128)(2,1)S(1)} %copy-done.4, f32[128]{0:T(128)S(1)} %copy-done.23, f32[128]{0:T(128)S(1)} %copy-done.21, f32[2048]{0:T(1024)S(1)} %bitcast.281, f32[128,2048]{1,0:T(8,128)} %fusion.80, ...), kind=kOutput, calls=%fused_computation.96 | convolution fusion | flops 4297846784 | bytes 38299648 | tf_op jit(solution)/shard_map/dot_general | solution.py:45
  1310.6 43.6 %all-reduce.9 = (bf16[2048]{0:T(1024)(128)(2,1)S(1)}, bf16[2048]{0:T(1024)(128)(2,1)S(1)}, bf16[6144]{0:T(1024)(128)(2,1)S(1)}, bf16[2048]{0:T(1024)(128)(2,1)S(1)}, bf16[8192]{0:T(1024)(128)(2,1)S(1)}) all-reduce(f32[2048]{0:T(1024)S(1)} %reshape.440, ...), channel_id=3, replica_groups=mesh['seq'=8,'fsdp'=4] {'seq','fsdp'}, use_global_device_ids=true, to_apply=%region_12.13.clone | all-reduce | flops 20480 | bytes 122880
  1355.5 15.7 %all-reduce.10 = (bf16[512]{0:T(512)(128)(2,1)S(1)}, bf16[512]{0:T(512)(128)(2,1)S(1)}, bf16[1536]{0:T(1024)(128)(2,1)S(1)}, bf16[512]{0:T(512)(128)(2,1)S(1)}) all-reduce(bf16[512]{0:T(512)(128)(2,1)S(1)} %dynamic-update-slice, bf16[512]{0:T(512)(128)(2,1)S(1)} %dynamic-update-slice.1, ...), channel_id=1, replica_groups=mesh['seq'=8,'fsdp'=4] {'seq'}, use_global_device_ids=true, to_apply=%add | all-reduce | flops 3072 | bytes 12288
  1385.2 14.4 fusion.53
  1408.9 19.1 %all-gather.32.cloned.1.call-done = bf16[512,8192]{1,0:T(8,128)(2,1)} async-done(((bf16[512,1024]{1,0:T(8,128)(2,1)}), bf16[512,8192]{1,0:T(8,128)(2,1)}) %all-gather.32.cloned.1.call-update) | async-done | bytes 8388624 | tf_op jit(solution)/shard_map/all_gather | solution.py:348
  1428.0 12.5 convert_element_type.217
  1440.5 69.5 %all-gather.34.cloned.1.call-done = bf16[2048,2048]{1,0:T(8,128)(2,1)} async-done(((bf16[256,2048]{1,0:T(8,128)(2,1)}), bf16[2048,2048]{1,0:T(8,128)(2,1)}) %all-gather.34.cloned.1.call-update) | async-done | bytes 8388624 | tf_op jit(solution)/shard_map/all_gather | solution.py:351
  1510.0 11.7 convert_element_type.222
  (289 shorter events, 300.9 us)
Async XLA Ops:
  7.2 93.1 %all-gather.20.cloned.1.call-start = ((), (), s32[]{:S(2)}) async-start(), calls=%async_computation.13 | async-start | bytes 10485760 | tf_op jit(solution)/shard_map/all_gather | solution.py:158
  7.9 321.8 %all-gather.18.cloned.1.call-start = ((), (), s32[]{:S(2)}) async-start(), calls=%async_computation.12 | async-start | bytes 31457280 | tf_op jit(solution)/shard_map/all_gather | solution.py:157
  8.7 598.8 %all-gather.36.cloned.1.call-start = ((), (), s32[]{:S(2)}) async-start(), calls=%async_computation.25 | async-start | bytes 4718592 | tf_op jit(solution)/shard_map/all_gather | solution.py:290
  9.4 634.9 %all-gather.26.cloned.1.call-start = ((), (), s32[]{:S(2)}) async-start(), calls=%async_computation.16 | async-start | bytes 4718592 | tf_op jit(solution)/shard_map/all_gather | solution.py:289
  29.6 721.7 %all-gather.22.cloned.1.call-start = ((), (), s32[]{:S(2)}) async-start(), calls=%async_computation.14 | async-start | bytes 41943040 | tf_op jit(solution)/shard_map/all_gather | solution.py:159
  30.2 1019.9 %all-gather.24.cloned.1.call-start = ((), (), s32[]{:S(2)}) async-start(), calls=%async_computation.15 | async-start | bytes 41943040 | tf_op jit(solution)/shard_map/all_gather | solution.py:160
  39.4 290.4 %copy-start.9 = (bf16[128,2048]{1,0:T(8,128)(2,1)S(1)}, bf16[128,2048]{1,0:T(8,128)(2,1)}, u32[]{:S(2)}) copy-start(bf16[128,2048]{1,0:T(8,128)(2,1)} %fusion.64) | copy-start | bytes 1572868
  107.4 240.2 %all-to-all-start.2 = ((bf16[128,8,256]{2,0,1:T(8,128)(2,1)}), bf16[128,8,256]{2,0,1:T(8,128)(2,1)}, u32[]{:S(2)}, u32[]{:S(2)}) async-start(bf16[128,8,256]{2,0,1:T(8,128)(2,1)} %bitcast.210), calls=%async_computation.2 | async-start | bytes 1048576 | tf_op jit(solution)/shard_map/all_to_all | solution.py:240
  347.6 63.0 %all-to-all-start = ((bf16[128,3,8,256]{0,3,1,2:T(8,128)(2,1)}), bf16[128,3,8,256]{0,3,1,2:T(8,128)(2,1)}, u32[]{:S(2)}, u32[]{:S(2)}) async-start(bf16[128,3,8,256]{0,3,1,2:T(8,128)(2,1)} %copy.106), calls=%async_computation | async-start | bytes 3145728 | tf_op jit(solution)/shard_map/all_to_all | solution.py:198
  457.1 71.6 %all-to-all-start.1 = ((bf16[8,2,16384]{2,1,0:T(2,128)(2,1)}), bf16[8,2,16384]{2,1,0:T(2,128)(2,1)}, u32[]{:S(2)}, u32[]{:S(2)}) async-start(bf16[8,2,16384]{2,1,0:T(2,128)(2,1)} %reshape.497), calls=%async_computation.1 | async-start | bytes 1048576 | tf_op jit(solution)/shard_map/all_to_all | solution.py:204
  528.8 54.0 %all-to-all-start.3 = ((bf16[1024,3,1,256]{3,1,2,0:T(4,128)(2,1)}), bf16[1024,3,1,256]{3,1,2,0:T(4,128)(2,1)S(1)}, u32[]{:S(2)}, u32[]{:S(2)}) async-start(bf16[1024,3,1,256]{3,1,2,0:T(4,128)(2,1)} %copy.114), calls=%async_computation.3 | async-start | bytes 4194304 | tf_op jit(solution)/shard_map/all_to_all | solution.py:256
  582.8 19.5 %all-to-all-start.5 = ((bf16[128,4,8,64]{0,3,1,2:T(8,128)(2,1)}), bf16[128,4,8,64]{0,3,1,2:T(8,128)(2,1)}, u32[]{:S(2)}, u32[]{:S(2)}) async-start(bf16[128,4,8,64]{0,3,1,2:T(8,128)(2,1)} %copy.122), calls=%async_computation.6 | async-start | bytes 1048576 | tf_op jit(solution)/shard_map/all_to_all | solution.py:311
  602.3 41.3 %all-to-all-start.4 = ((bf16[128,8,768]{0,2,1:T(8,128)(2,1)}), bf16[128,8,768]{0,2,1:T(8,128)(2,1)S(1)}, u32[]{:S(2)}, u32[]{:S(2)}) async-start(bf16[128,8,768]{0,2,1:T(8,128)(2,1)} %bitcast.37), calls=%async_computation.4 | async-start | bytes 3145728 | tf_op jit(solution)/shard_map/all_to_all | solution.py:293
  605.9 591.2 %reduce-scatter.7.cloned.1.call-start = ((), (), s32[]{:S(2)}) async-start(), calls=%async_computation.19 | async-start | bytes 1310720 | tf_op jit(solution)/shard_map/reduce_scatter | solution.py:330
  612.0 585.8 %reduce-scatter.5.cloned.1.call-start = ((), (), s32[]{:S(2)}) async-start(), calls=%async_computation.17 | async-start | bytes 3932160 | tf_op jit(solution)/shard_map/reduce_scatter | solution.py:330
  644.3 107.0 %copy-start.10 = (bf16[128,2048]{1,0:T(8,128)(2,1)S(1)}, bf16[128,2048]{1,0:T(8,128)(2,1)}, u32[]{:S(2)}) copy-start(bf16[128,2048]{1,0:T(8,128)(2,1)} %fusion.64) | copy-start | bytes 1572868
  651.8 398.3 %copy-start.12 = (bf16[1,128,2048]{2,1,0:T(8,128)(2,1)S(1)}, bf16[1,128,2048]{2,1,0:T(8,128)(2,1)}, u32[]{:S(2)}) copy-start(bf16[1,128,2048]{2,1,0:T(8,128)(2,1)} %param.31) | copy-start | bytes 1572868
  651.8 546.5 %reduce-scatter.9.cloned.1.call-start = ((), (), s32[]{:S(2)}) async-start(), calls=%async_computation.21 | async-start | bytes 5242880 | tf_op jit(solution)/shard_map/reduce_scatter | solution.py:330
  1128.3 119.4 %reduce-scatter.11.cloned.1.call-start = ((), (), s32[]{:S(2)}) async-start(), calls=%async_computation.23 | async-start | bytes 5242880 | tf_op jit(solution)/shard_map/reduce_scatter | solution.py:330
  1197.0 88.2 %all-gather.30.cloned.1.call-start = ((), (), s32[]{:S(2)}) async-start(), calls=%async_computation.20 | async-start | bytes 2359296 | tf_op jit(solution)/shard_map/all_gather | solution.py:345
  1197.7 201.9 %all-gather.28.cloned.1.call-start = ((), (), s32[]{:S(2)}) async-start(), calls=%async_computation.18 | async-start | bytes 7077888 | tf_op jit(solution)/shard_map/all_gather | solution.py:342
  1198.3 229.7 %all-gather.32.cloned.1.call-start = ((), (), s32[]{:S(2)}) async-start(), calls=%async_computation.22 | async-start | bytes 9437184 | tf_op jit(solution)/shard_map/all_gather | solution.py:348
  1199.1 310.9 %all-gather.34.cloned.1.call-start = ((), (), s32[]{:S(2)}) async-start(), calls=%async_computation.24 | async-start | bytes 9437184 | tf_op jit(solution)/shard_map/all_gather | solution.py:351
  1371.8 149.9 %copy-start.19 = (f32[512]{0:T(512)}, f32[512]{0:T(512)S(1)}, u32[]{:S(2)}) copy-start(f32[512]{0:T(512)S(1)} %convert_element_type.215) | copy-start | bytes 6148
  (38 other events, 783.0 us)
Sparse Core Ops, SparseCore 0:
  9.9 90.3 all-gather.19
  102.2 227.5 all-gather.17
  331.4 74.1 all-gather.35
  407.6 45.9 all-gather.25
  455.2 296.0 all-gather.21
  753.0 297.0 all-gather.23
  1053.6 27.9 reduce-scatter.6
  1085.1 43.8 reduce-scatter.4
  1132.6 52.5 reduce-scatter.8
  1197.1 50.5 reduce-scatter.10
  1249.3 29.1 all-gather.29
  1279.9 64.8 all-gather.27
  1346.4 81.4 all-gather.31
  1429.4 80.4 all-gather.33
where the time goes:
time: 1540 us; the launch traced here: 1530 us
  waiting for transfers between devices  930 us (60%)
  blocking collectives  227 us (15%)
  matrix products  184 us (12%)
  other arithmetic  69 us (4%)
  local copies, waits for them, and re-layouts  68.4 us (4%)
  starting transfers between devices  27.6 us (2%)
  between operations  16.1 us (1%)
    all_gather x1, waiting for transfers between devices, body(): lax.all_gather(fc2_weight, 'fsdp', axis=0, tiled=True)  280 us
    all_gather x1, waiting for transfers between devices, body(): lax.all_gather(qkv_weight, 'fsdp', axis=0, tiled=True)  218 us
    all_gather x1, waiting for transfers between devices, body(): lax.all_gather(fc1_weight, 'fsdp', axis=0, tiled=True)  99.4 us
    all_gather x1, waiting for transfers between devices, body(): lax.all_gather(piece_down.astype(jnp.bfloat16), 'seq', axis=0, tiled=True)  69.5 us
    all_gather x1, waiting for transfers between devices, body(): lax.all_gather(dense_weight, 'fsdp', axis=0, tiled=True)  60.9 us
    unnamed x2, blocking collectives  59.4 us
    all_to_all x1, waiting for transfers between devices, body(): lax.all_to_all(outgoing, 'seq', split_axis=2, concat_axis=0, tiled=True)  56.5 us
    dot_general x4, matrix products, contract_cols(): lax.dot_general(left_side, right_side, (((1,), (1,)), ((), ())), preferre...  56.2 us
  transfers between devices with their start and end apart: 20, of which 11 were waited for; matrix products, arithmetic and copies ran while one was open for 20% of the time, Pallas kernels for 0%

commit v1 on v0

--- a/solution.py
+++ b/solution.py
@@ -7,6 +7,18 @@
 HEAD = 64
 ROT = 32
 norm_epsilon = 1e-05
+
+
+def doubled_up(x, axis, dim):
+    ways, here = (lax.axis_size(axis), lax.axis_index(axis))
+    grown, reach = (x, 1)
+    while reach < ways:
+        theirs = lax.ppermute(grown, axis, [(d, d ^ reach) for d in range(ways)])
+        mine_first = jnp.concatenate([grown, theirs], axis=dim)
+        theirs_first = jnp.concatenate([theirs, grown], axis=dim)
+        grown = jnp.where(here & reach == 0, mine_first, theirs_first)
+        reach = 2 * reach
+    return grown
 
 
 def rotary_angles(pos_row, rot_width):
@@ -154,7 +166,7 @@
     seq_count = lax.axis_size("seq")
     shard_count = lax.axis_size("fsdp")
     gathered = (
-        lax.all_gather(qkv_weight, "fsdp", axis=0, tiled=True),
+        doubled_up(qkv_weight, "fsdp", 0),
         lax.all_gather(dense_weight, "fsdp", axis=0, tiled=True),
         lax.all_gather(fc1_weight, "fsdp", axis=0, tiled=True),
         lax.all_gather(fc2_weight, "fsdp", axis=0, tiled=True),

time: 1540 us -> 1810 us (1.18)
  blocking collectives: 227 us -> 722 us
  waiting for transfers between devices: 930 us -> 675 us
  other arithmetic: 69 us -> 88.4 us
    all_gather x1, blocking collectives: 7.71 us -> 508 us  [body(): lax.all_gather(qkv_bias, 'fsdp', axis=0, tiled=True)]
    all_gather x1, waiting for transfers between devices: 280 us -> 0.01 us  [body(): lax.all_gather(fc2_weight, 'fsdp', axis=0, tiled=True)]
    ppermute x0 -> x2, waiting for transfers between devices: none -> 192 us  [doubled_up(): theirs = lax.ppermute(grown, axis, [(d, d ^ reach) for d in range(ways)])]
    all_gather x1, waiting for transfers between devices: 99.4 us -> 0.02 us  [body(): lax.all_gather(fc1_weight, 'fsdp', axis=0, tiled=True)]
    all_gather x1, waiting for transfers between devices: 60.9 us -> 0.01 us  [body(): lax.all_gather(dense_weight, 'fsdp', axis=0, tiled=True)]
    all_gather x1, waiting for transfers between devices: 0.01 us -> 52 us  [body(): lax.all_gather(piece_qkv.astype(jnp.bfloat16), 'seq', axis=1, tiled=True)]
    all_gather x1, waiting for transfers between devices: 69.5 us -> 35.8 us  [body(): lax.all_gather(piece_down.astype(jnp.bfloat16), 'seq', axis=0, tiled=True)]
    all_to_all x1, waiting for transfers between devices: 56.5 us -> 36 us  [body(): lax.all_to_all(outgoing, 'seq', split_axis=2, concat_axis=0, tiled=True)]
  transfers between devices with their start and end apart: 20 -> 22, of which waited for: 11 -> 10; matrix products, arithmetic and copies ran while one was open for 20% -> 18% of each run, Pallas kernels for 0% -> 0%
where the time goes in v1:
time: 1810 us; the launch traced here: 1800 us
  blocking collectives  722 us (40%)
  waiting for transfers between devices  675 us (37%)
  matrix products  187 us (10%)
  other arithmetic  88.4 us (5%)
  local copies, waits for them, and re-layouts  72 us (4%)
  starting transfers between devices  29.9 us (2%)
    all_gather x1, blocking collectives, body(): lax.all_gather(qkv_bias, 'fsdp', axis=0, tiled=True)  508 us
    all_gather x1, waiting for transfers between devices, body(): lax.all_gather(qkv_weight, 'fsdp', axis=0, tiled=True)  225 us
    ppermute x2, waiting for transfers between devices, doubled_up(): theirs = lax.ppermute(grown, axis, [(d, d ^ reach) for d in range(ways)])  192 us
    unnamed x2, blocking collectives  59.4 us
    dot_general x4, matrix products, contract_cols(): lax.dot_general(left_side, right_side, (((1,), (1,)), ((), ())), preferre...  56.7 us
    all_to_all x1, blocking collectives, body(): lax.all_to_all(activated.reshape(tok_len, shard_count, seq_count, row_dow...  52.8 us
    all_gather x1, waiting for transfers between devices, body(): lax.all_gather(piece_qkv.astype(jnp.bfloat16), 'seq', axis=1, tiled=True)  52 us
    all_to_all x1, blocking collectives, body(): lax.all_to_all(grad_pre.reshape(tok_len, seq_count, col_up), 'seq', split...  51.7 us
  transfers between devices with their start and end apart: 22, of which 10 were waited for; matrix products, arithmetic and copies ran while one was open for 18% of the time, Pallas kernels for 0%

profile of v1, /device:TPU:0, one launch (start us, length us, event | category | flops | bytes accessed | tf_op | source)
XLA Modules:
  0.0 1797.9 jit_solution(5753024446363257602)
XLA Ops:
  35.0 191.6 %collective-permute-done = bf16[512,6144]{1,0:T(8,128)(2,1)} collective-permute-done((bf16[512,6144]{1,0:T(8,128)(2,1)}, bf16[512,6144]{1,0:T(8,128)(2,1)}, u32[]{:S(2)}, u32[]{:S(2)}) %collective-permute-start) | collective-permute-done | bytes 6291488 | tf_op jit(solution)/shard_map/ppermute | solution.py:16
  226.7 15.9 maximum_select_fusion.2
  244.0 508.4 %all-gather.3 = bf16[4,1,1536]{2,1,0:T(2,128)(2,1)S(1)} all-gather(bf16[1,1,1536]{2,1,0:T(2,128)(2,1)S(1)} %reshape.474), channel_id=1, replica_groups=mesh['seq'=8,'fsdp'=4] {'fsdp'}, dimensions={0}, use_global_device_ids=true | all-gather | bytes 15360 | tf_op jit(solution)/shard_map/all_gather | solution.py:175
  764.7 20.0 %fusion.40 = f32[128,6144]{1,0:T(8,128)} fusion(bf16[128,2048]{1,0:T(8,128)(2,1)S(1)} %copy-done.11, bf16[1024,6144]{1,0:T(8,128)(2,1)} %collective-permute-done.1, bf16[1024,6144]{1,0:T(8,128)(2,1)} %maximum_select_fusion.2, pred[]{:T(512)S(6)} %eq.44, f32[6144]{0:T(1024)S(1)} %bitcast.292), kind=kOutput, calls=%fused_computation.53 | convolution fusion | flops 3335258112 | bytes 28860416 | tf_op jit(solution)/shard_map/dot_general | solution.py:201
  796.4 36.0 %all-to-all-done = bf16[128,3,8,256]{0,3,1,2:T(8,128)(2,1)} async-done(((bf16[128,3,8,256]{0,3,1,2:T(8,128)(2,1)}), bf16[128,3,8,256]{0,3,1,2:T(8,128)(2,1)}, u32[]{:S(2)}, u32[]{:S(2)}) %all-to-all-start) | async-done | bytes 1572896 | tf_op jit(solution)/shard_map/all_to_all | solution.py:210
  843.0 20.8 %while.27 = (s32[]{:T(128)}, bf16[2,512,4,64]{1,3,2,0:T(8,128)(2,1)}, f32[2,4,512]{2,1,0:T(4,128)S(1)}, s32[2]{0:T(128)S(1)}, s32[1024]{0:T(1024)S(1)}, /*index=...) while((s32[]{:T(128)}, ...), condition=%wide.region_5.6_spmd, body=%wide.region_2.5_spmd.sunk | while | flops 563608064 | bytes 31275748 | solution.py:100
  884.4 62.4 %while.28 = (s32[]{:T(128)}, f32[1024,4,64]{0,2,1:T(8,128)S(1)}, f32[1024,4,64]{0,2,1:T(8,128)S(1)}, bf16[2,512,4,64]{1,3,2,0:T(8,128)(2,1)}, s32[2]{0:T(128)S(1...) while((s32[]{:T(128)}, f32[1024,4,64]{0,2,1:T(8,128)S(1)}, ...), condition=%wide.region_8.9_spmd.clone, body=%wide.region_6.8_spmd.clone.sunk | while | flops 1366161920 | bytes 180411312 | solution.py:144
  962.0 43.7 %all-to-all-done.3 = bf16[1024,3,1,256]{3,1,2,0:T(4,128)(2,1)S(1)} async-done(((bf16[1024,3,1,256]{3,1,2,0:T(4,128)(2,1)}), bf16[1024,3,1,256]{3,1,2,0:T(4,128)(2,1)S(1)}, u32[]{:S(2)}, u32[]{:S(2)}) %all-to-all-start.3) | async-done | bytes 1572896 | tf_op jit(solution)/shard_map/all_to_all | solution.py:268
  1042.6 24.0 %all-to-all-done.4 = bf16[128,8,768]{0,2,1:T(8,128)(2,1)S(1)} async-done(((bf16[128,8,768]{0,2,1:T(8,128)(2,1)}), bf16[128,8,768]{0,2,1:T(8,128)(2,1)S(1)}, u32[]{:S(2)}, u32[]{:S(2)}) %all-to-all-start.4) | async-done | bytes 1572896 | tf_op jit(solution)/shard_map/all_to_all | solution.py:305
  1075.0 16.4 multiply_convert_fusion.1
  1091.4 18.2 %convert_reduce_fusion = (f32[8192]{0:T(1024)S(1)}, bf16[128,8192]{1,0:T(8,128)(2,1)S(1)}) fusion(f32[128,8192]{1,0:T(8,128)} %get-tuple-element.255, bf16[8192,2048]{1,0:T(8,128)(2,1)} %all-gather.22.cloned.1.call-done, bf16[1,128,2048]{2,1,0:T(8,128)(2,1)S(1)} %copy-done.9), kind=kOutput, calls=%fused_computation.67 | convolution fusion | flops 4318027776 | bytes 40402944 | tf_op jit(solution)/shard_map/dot_general | solution.py:57
  1109.8 51.7 %all_to_all.114 = bf16[128,8,1024]{2,0,1:T(8,128)(2,1)S(1)} all-to-all(bf16[128,8,1024]{2,0,1:T(8,128)(2,1)S(1)} %bitcast.255), channel_id=1, replica_groups=mesh['seq'=8,'fsdp'=4] {'seq'}, dimensions={1} | all-to-all | bytes 4194304 | tf_op jit(solution)/shard_map/all_to_all | solution.py:312
  1175.9 52.8 %all_to_all.115 = bf16[128,4,8,256]{0,3,1,2:T(8,128)(2,1)S(1)} all-to-all(bf16[128,4,8,256]{0,3,1,2:T(8,128)(2,1)} %copy.127), channel_id=1, replica_groups=mesh['seq'=8,'fsdp'=4] {'seq'}, dimensions={2} | all-to-all | bytes 4194304 | tf_op jit(solution)/shard_map/all_to_all | solution.py:330
  1238.9 48.5 %reduce-scatter.11.cloned.1.call-done = bf16[256,2048]{1,0:T(8,128)(2,1)} async-done(((bf16[1024,2048]{1,0:T(8,128)(2,1)}), bf16[256,2048]{1,0:T(8,128)(2,1)}) %reduce-scatter.11.cloned.1.call-update) | async-done | bytes 1048592 | tf_op jit(solution)/shard_map/reduce_scatter | solution.py:342
  1322.2 224.7 %all-gather.24.cloned.1.call-done = bf16[2048,6144]{1,0:T(8,128)(2,1)} async-done(((bf16[512,6144]{1,0:T(8,128)(2,1)}), bf16[2048,6144]{1,0:T(8,128)(2,1)}) %all-gather.24.cloned.1.call-update) | async-done | bytes 25165840 | tf_op jit(solution)/shard_map/all_gather | solution.py:234
  1547.0 14.2 fusion.89
  1561.2 52.0 %all-gather.28.cloned.1.call-done = bf16[512,6144]{1,0:T(8,128)(2,1)} async-done(((bf16[512,768]{1,0:T(8,128)(2,1)}), bf16[512,6144]{1,0:T(8,128)(2,1)}) %all-gather.28.cloned.1.call-update) | async-done | bytes 6291472 | tf_op jit(solution)/shard_map/all_gather | solution.py:354
  1622.9 18.0 %fusion.76 = (f32[2048]{0:T(1024)S(1)}, f32[128]{0:T(128)S(1)}, f32[128]{0:T(128)S(1)}, f32[2048]{0:T(1024)S(1)}, f32[128,2048]{1,0:T(8,128)}) fusion(bf16[1,128,2048]{2,1,0:T(8,128)(2,1)S(1)} %copy-done.3, f32[128]{0:T(128)S(1)} %copy-done.22, f32[128]{0:T(128)S(1)} %copy-done.20, f32[2048]{0:T(1024)S(1)} %bitcast.280, f32[128,2048]{1,0:T(8,128)} %fusion.89, ...), kind=kOutput, calls=%fused_computation.105 | convolution fusion | flops 4297846784 | bytes 38299648 | tf_op jit(solution)/shard_map/dot_general | solution.py:57
  1644.4 44.4 %all-reduce.9 = (bf16[2048]{0:T(1024)(128)(2,1)S(1)}, bf16[2048]{0:T(1024)(128)(2,1)S(1)}, bf16[6144]{0:T(1024)(128)(2,1)S(1)}, bf16[2048]{0:T(1024)(128)(2,1)S(1)}, bf16[8192]{0:T(1024)(128)(2,1)S(1)}) all-reduce(f32[2048]{0:T(1024)S(1)} %reshape.440, ...), channel_id=3, replica_groups=mesh['seq'=8,'fsdp'=4] {'seq','fsdp'}, use_global_device_ids=true, to_apply=%region_12.13.clone | all-reduce | flops 20480 | bytes 122880
  1690.1 15.0 all-reduce.10
  1716.7 14.4 fusion.61
  1731.1 11.8 convert_element_type.217
  1742.9 35.8 %all-gather.34.cloned.1.call-done = bf16[2048,2048]{1,0:T(8,128)(2,1)} async-done(((bf16[256,2048]{1,0:T(8,128)(2,1)}), bf16[2048,2048]{1,0:T(8,128)(2,1)}) %all-gather.34.cloned.1.call-update) | async-done | bytes 8388624 | tf_op jit(solution)/shard_map/all_gather | solution.py:363
  1778.6 11.7 convert_element_type.222
  (288 shorter events, 305.6 us)
Async XLA Ops:
  7.2 746.0 %all-gather.18.cloned.1.call-start = ((), (), s32[]{:S(2)}) async-start(), calls=%async_computation.12 | async-start | bytes 10485760 | tf_op jit(solution)/shard_map/all_gather | solution.py:170
  7.9 1022.4 %all-gather.36.cloned.1.call-start = ((), (), s32[]{:S(2)}) async-start(), calls=%async_computation.25 | async-start | bytes 4718592 | tf_op jit(solution)/shard_map/all_gather | solution.py:302
  8.7 1058.6 %all-gather.26.cloned.1.call-start = ((), (), s32[]{:S(2)}) async-start(), calls=%async_computation.16 | async-start | bytes 4718592 | tf_op jit(solution)/shard_map/all_gather | solution.py:301
  33.3 1041.7 %all-gather.20.cloned.1.call-start = ((), (), s32[]{:S(2)}) async-start(), calls=%async_computation.13 | async-start | bytes 41943040 | tf_op jit(solution)/shard_map/all_gather | solution.py:171
  33.9 1057.6 %all-gather.22.cloned.1.call-start = ((), (), s32[]{:S(2)}) async-start(), calls=%async_computation.14 | async-start | bytes 41943040 | tf_op jit(solution)/shard_map/all_gather | solution.py:172
  34.4 192.2 %collective-permute-start = (bf16[512,6144]{1,0:T(8,128)(2,1)}, bf16[512,6144]{1,0:T(8,128)(2,1)}, u32[]{:S(2)}, u32[]{:S(2)}) collective-permute-start(bf16[512,6144]{1,0:T(8,128)(2,1)} %param.21), channel_id=1, source_target_pairs={{0,1},{1,0},{2,3},{3,2},{4,5},{5,4},{6,7},{7,6},{8,9},{9,8},{10,11... | collective-permute-start | bytes 18874376 | tf_op jit(solution)/shard_map/ppermute | solution.py:16
  35.0 717.4 %copy-start.29 = (s32[1,128]{1,0:T(1,128)S(1)}, s32[1,128]{1,0:T(1,128)}, u32[]{:S(2)}) copy-start(s32[1,128]{1,0:T(1,128)} %param.30) | copy-start | bytes 1540
  35.0 718.2 %copy-start.8 = (bf16[1,128,2048]{2,1,0:T(8,128)(2,1)S(1)}, bf16[1,128,2048]{2,1,0:T(8,128)(2,1)}, u32[]{:S(2)}) copy-start(bf16[1,128,2048]{2,1,0:T(8,128)(2,1)} %param.31) | copy-start | bytes 1572868
  242.5 522.2 %collective-permute-start.1 = (bf16[1024,6144]{1,0:T(8,128)(2,1)}, bf16[1024,6144]{1,0:T(8,128)(2,1)}, u32[]{:S(2)}, u32[]{:S(2)}) collective-permute-start(bf16[1024,6144]{1,0:T(8,128)(2,1)} %maximum_select_fusion.2), channel_id=1, source_target_pairs={{0,2},{1,3},{2,0},{3,1},{4,6},{5,7},{6,4},{7,5},{8,10},{9,11},{10,... | collective-permute-start | bytes 37748744 | tf_op jit(solution)/shard_map/ppermute | solution.py:16
  760.3 28.9 %all-to-all-start.2 = ((bf16[128,8,256]{2,0,1:T(8,128)(2,1)}), bf16[128,8,256]{2,0,1:T(8,128)(2,1)}, u32[]{:S(2)}, u32[]{:S(2)}) async-start(bf16[128,8,256]{2,0,1:T(8,128)(2,1)} %bitcast.209), calls=%async_computation.2 | async-start | bytes 1048576 | tf_op jit(solution)/shard_map/all_to_all | solution.py:252
  789.2 43.2 %all-to-all-start = ((bf16[128,3,8,256]{0,3,1,2:T(8,128)(2,1)}), bf16[128,3,8,256]{0,3,1,2:T(8,128)(2,1)}, u32[]{:S(2)}, u32[]{:S(2)}) async-start(bf16[128,3,8,256]{0,3,1,2:T(8,128)(2,1)} %copy.106), calls=%async_computation | async-start | bytes 3145728 | tf_op jit(solution)/shard_map/all_to_all | solution.py:210
  879.0 72.7 %all-to-all-start.1 = ((bf16[8,2,16384]{2,1,0:T(2,128)(2,1)}), bf16[8,2,16384]{2,1,0:T(2,128)(2,1)}, u32[]{:S(2)}, u32[]{:S(2)}) async-start(bf16[8,2,16384]{2,1,0:T(2,128)(2,1)} %reshape.497), calls=%async_computation.1 | async-start | bytes 1048576 | tf_op jit(solution)/shard_map/all_to_all | solution.py:216
  951.7 54.1 %all-to-all-start.3 = ((bf16[1024,3,1,256]{3,1,2,0:T(4,128)(2,1)}), bf16[1024,3,1,256]{3,1,2,0:T(4,128)(2,1)S(1)}, u32[]{:S(2)}, u32[]{:S(2)}) async-start(bf16[1024,3,1,256]{3,1,2,0:T(4,128)(2,1)} %copy.114), calls=%async_computation.3 | async-start | bytes 4194304 | tf_op jit(solution)/shard_map/all_to_all | solution.py:268
  1005.7 19.5 %all-to-all-start.5 = ((bf16[128,4,8,64]{0,3,1,2:T(8,128)(2,1)}), bf16[128,4,8,64]{0,3,1,2:T(8,128)(2,1)}, u32[]{:S(2)}, u32[]{:S(2)}) async-start(bf16[128,4,8,64]{0,3,1,2:T(8,128)(2,1)} %copy.122), calls=%async_computation.6 | async-start | bytes 1048576 | tf_op jit(solution)/shard_map/all_to_all | solution.py:323
  1025.2 41.3 %all-to-all-start.4 = ((bf16[128,8,768]{0,2,1:T(8,128)(2,1)}), bf16[128,8,768]{0,2,1:T(8,128)(2,1)S(1)}, u32[]{:S(2)}, u32[]{:S(2)}) async-start(bf16[128,8,768]{0,2,1:T(8,128)(2,1)} %bitcast.37), calls=%async_computation.4 | async-start | bytes 3145728 | tf_op jit(solution)/shard_map/all_to_all | solution.py:305
  1028.8 207.4 %reduce-scatter.7.cloned.1.call-start = ((), (), s32[]{:S(2)}) async-start(), calls=%async_computation.19 | async-start | bytes 1310720 | tf_op jit(solution)/shard_map/reduce_scatter | solution.py:342
  1034.7 202.9 %reduce-scatter.5.cloned.1.call-start = ((), (), s32[]{:S(2)}) async-start(), calls=%async_computation.17 | async-start | bytes 3932160 | tf_op jit(solution)/shard_map/reduce_scatter | solution.py:342
  1074.8 163.5 %reduce-scatter.9.cloned.1.call-start = ((), (), s32[]{:S(2)}) async-start(), calls=%async_computation.21 | async-start | bytes 5242880 | tf_op jit(solution)/shard_map/reduce_scatter | solution.py:342
  1167.8 119.7 %reduce-scatter.11.cloned.1.call-start = ((), (), s32[]{:S(2)}) async-start(), calls=%async_computation.23 | async-start | bytes 5242880 | tf_op jit(solution)/shard_map/reduce_scatter | solution.py:342
  1236.2 81.9 %all-gather.30.cloned.1.call-start = ((), (), s32[]{:S(2)}) async-start(), calls=%async_computation.20 | async-start | bytes 2359296 | tf_op jit(solution)/shard_map/all_gather | solution.py:357
  1236.8 310.1 %all-gather.24.cloned.1.call-start = ((), (), s32[]{:S(2)}) async-start(), calls=%async_computation.15 | async-start | bytes 31457280 | tf_op jit(solution)/shard_map/all_gather | solution.py:234
  1237.6 375.6 %all-gather.28.cloned.1.call-start = ((), (), s32[]{:S(2)}) async-start(), calls=%async_computation.18 | async-start | bytes 7077888 | tf_op jit(solution)/shard_map/all_gather | solution.py:354
  1238.2 492.9 %all-gather.32.cloned.1.call-start = ((), (), s32[]{:S(2)}) async-start(), calls=%async_computation.22 | async-start | bytes 9437184 | tf_op jit(solution)/shard_map/all_gather | solution.py:360
  1238.9 539.7 %all-gather.34.cloned.1.call-start = ((), (), s32[]{:S(2)}) async-start(), calls=%async_computation.24 | async-start | bytes 9437184 | tf_op jit(solution)/shard_map/all_gather | solution.py:363
  (37 other events, 1175.6 us)
Sparse Core Ops, SparseCore 0:
  9.8 147.7 all-gather.17
  159.2 46.8 all-gather.35
  208.3 45.6 all-gather.25
  255.7 527.8 all-gather.19
  785.2 297.2 all-gather.21
  1085.9 27.9 reduce-scatter.6
  1117.4 43.8 reduce-scatter.4
  1167.9 50.9 reduce-scatter.8
  1236.3 51.1 reduce-scatter.10
  1288.9 29.1 all-gather.29
  1320.0 226.9 all-gather.23
  1548.4 64.6 all-gather.27
  1614.8 81.7 all-gather.31
  1698.0 80.5 all-gather.33
